TPU v7x, 8 devices: a whole 2x2x1 slice. The times are simulated.
8 devices in a mesh: dp: 1 (over z), sp: 8 (over x, y, core).
Axes of the slice: x: 2, y: 2, z: 1, core: 2. Of those that a mesh axis runs over, the one named last changes fastest.
Arguments:
- q: bfloat16 [32, 32, 64], P('dp')
- k: bfloat16 [32, 4096, 32, 64], P('dp', 'sp')
- v: bfloat16 [32, 4096, 32, 64], P('dp', 'sp')
Outputs:
- q: bfloat16 [32, 32, 64], P('dp')
All inputs are finite; a program needn't handle non-finite values.
Results may differ from a plain program's by a relative error of at most 0.012.
Values are sent between devices in bfloat16 or wider.
A program may use at most 2 GiB of HBM per device.

v0:
```python
import jax
import jax.numpy as jnp
from jax import lax
from jax.sharding import PartitionSpec as P


def einsum(form, a, b):
    return jnp.einsum(form, a.astype(jnp.float32), b.astype(jnp.float32))


def part_of(q, k, v):
    grouped = q.reshape(q.shape[0], k.shape[2], -1, q.shape[2])
    scores = einsum("bgsd,bugd->bgsu", grouped, k) * q.shape[2] ** -0.5
    high = jnp.max(scores, -1, keepdims=True)
    weights = jnp.exp(scores - high)
    seen = einsum("bgsu,bugd->bgsd", weights.astype(jnp.bfloat16), v)
    return jnp.concatenate([seen, jnp.sum(weights, -1, keepdims=True), high], -1)


def together(parts):
    seen, total, high = parts[..., :-2], parts[..., -2:-1], parts[..., -1:]
    scale = jnp.exp(high - jnp.max(high, 0))
    return (jnp.sum(seen * scale, 0) / jnp.sum(total * scale, 0)).astype(jnp.bfloat16)


def solution(mesh):
    def step(q, k, v):
        return together(lax.all_gather(part_of(q, k, v), "sp")).reshape(q.shape)

    return jax.shard_map(
        step,
        mesh=mesh,
        in_specs=(P("dp", None, None), P("dp", "sp", None, None), P("dp", "sp", None, None)),
        out_specs=P("dp", None, None),
        check_vma=False,
    )
```

profile of v0, /device:TPU:0, one launch (start us, length us, event | category | flops | bytes accessed | tf_op | source)
XLA Modules:
  0.0 113.6 jit_solution(4509433366174437672)
XLA Ops:
  6.5 0.0 all-gather.3.cloned.1.call-start
  6.5 22.7 %fusion.7 = f32[32,32,1,512]{3,2,1,0:T(1,128)S(1)} fusion(bf16[32,512,32,64]{1,3,2,0:T(8,128)(2,1)} %param.4, bf16[32,32,64,1]{2,1,0,3:T(8,128)(2,1)} %bitcast.26), kind=kOutput, calls=%fused_computation.12 | convolution fusion | flops 67108864 | bytes 69337088 | tf_op jit(solution)/shard_map/bgsd,bugd->bgsu/dot_general | solution.py:8
  29.3 0.2 fusion.5
  29.5 0.6 fusion.6
  30.1 0.3 copy.17
  30.4 0.3 copy.16
  30.6 25.6 %fusion.1 = f32[32,32,1,64]{3,2,1,0:T(1,128)S(1)} fusion(bf16[32,512,32,64]{1,3,2,0:T(8,128)(2,1)} %param.5, bf16[32,32,512,1]{2,1,0,3:T(8,128)(2,1)S(1)} %get-tuple-element.7), kind=kOutput, calls=%fused_computation.3 | convolution fusion | flops 67108864 | bytes 68419584 | tf_op jit(solution)/shard_map/bgsu,bugd->bgsd/dot_general | solution.py:8
  56.2 1.2 %pad_maximum_fusion = f32[32,32,1,66]{3,1,2,0:T(8,128)} fusion(f32[32,32,1,1]{3,1,2,0:T(8,128)S(1)} %copy.17, f32[32,32,1,1]{3,1,2,0:T(8,128)S(1)} %copy.16, f32[32,32,1,64]{3,1,2,0:T(8,128)S(1)} %bitcast.27), kind=kLoop, calls=%fused_computation.11 | loop fusion | flops 135168 | bytes 540672 | tf_op jit(solution)/shard_map/concatenate | solution.py:17
  57.4 0.0 all-gather.3.cloned.1.call-update
  57.4 33.7 %all-gather.3.cloned.1.call-done = f32[256,32,1,66]{3,1,2,0:T(8,128)} async-done(((f32[32,32,1,66]{3,1,2,0:T(8,128)}), f32[256,32,1,66]{3,1,2,0:T(8,128)}) %all-gather.3.cloned.1.call-update) | async-done | bytes 2162704 | tf_op jit(solution)/shard_map/all_gather | solution.py:28
  91.1 7.6 %copy.18 = f32[256,32,1,66]{1,0,3,2:T(8,128)} copy(f32[256,32,1,66]{3,1,2,0:T(8,128)} %all-gather.3.cloned.1.call-done) | data formatting | bytes 4325376 | tf_op jit(solution)/shard_map/all_gather | solution.py:28
  98.8 0.9 slice_reduce_fusion
  99.7 1.0 fusion.9
  100.7 4.7 %fusion = f32[32,32,64]{1,0,2:T(8,128)S(1)} fusion(f32[8,32,32,1,66]{2,1,0,4,3:T(8,128)} %bitcast.25, f32[8,32,32]{2,1,0:T(8,128)S(1)} %get-tuple-element.6), kind=kLoop, calls=%fused_computation.1 | loop fusion | flops 983040 | bytes 2392064 | tf_op jit(solution)/shard_map/reduce_sum | solution.py:23
  105.4 0.1 divide_convert_fusion
  105.5 1.3 %copy.19 = bf16[32,32,64]{2,1,0:T(8,128)(2,1)} copy(bf16[32,32,64]{1,0,2:T(8,128)(2,1)S(1)} %divide_convert_fusion) | data formatting | bytes 262144 | tf_op jit(solution)/shard_map/convert_element_type | solution.py:23
Async XLA Ops:
  6.5 84.6 %all-gather.3.cloned.1.call-start = ((), (), s32[]{:S(2)}) async-start(), calls=%async_computation | async-start | bytes 4718592 | tf_op jit(solution)/shard_map/all_gather | solution.py:28
Sparse Core Ops, SparseCore 0:
  57.5 33.5 all-gather.2
where the time goes:
time: 114 us
  matrix products  48.3 us (42%)
  waiting for transfers between devices  33.7 us (30%)
  between operations  13.4 us (12%)
  local copies, waits for them, and re-layouts  9.44 us (8%)
  other arithmetic  8.72 us (8%)
    dot_general x2, matrix products, einsum(): return jnp.einsum(form, a.astype(jnp.float32), b.astype(jnp.float32))  48.3 us
    all_gather x1, waiting for transfers between devices, step(): return together(lax.all_gather(part_of(q, k, v), 'sp')).reshape(q.shape)  33.7 us
    all_gather x1, local copies, waits for them, and re-layouts, step(): return together(lax.all_gather(part_of(q, k, v), 'sp')).reshape(q.shape)  7.62 us
    reduce_sum x1, other arithmetic, together(): jnp.sum(seen * scale, 0) / jnp.sum(total * scale, 0)  4.69 us
  transfers between devices with their start and end apart: 1, of which 1 were waited for; matrix products, arithmetic and copies ran while one was open for 0% of the time, Pallas kernels for 0%

commit v1 on v0

v1 whole, which is shorter than its diff:
```python
import functools

import jax
import jax.numpy as jnp
from jax import lax
from jax.experimental import pallas as pl
from jax.experimental.pallas import tpu as pltpu
from jax.sharding import PartitionSpec as P

MESH = pl.DeviceIdType.MESH
SLOTS = 6
LAG = 4
GROUP = 8
PEERS = [(x, y, c) for x in (1, 0) for y in (1, 0) for c in (1, 0)][:-1]


def attend(pairs, heads, head, q_hbm, k_hbm, v_hbm, out_ref, q_ref, kbuf, vbuf, weights, part, stat, parts, stats, qsem, ksem, vsem, send, recv):
    batch, groups, lanes = 2 * pairs, heads // GROUP, 2 * head
    tokens = kbuf.shape[2]
    me = lax.axis_index("sp")
    mx, my, mc = me // 4, (me // 2) % 2, me % 2
    devices = [((mx + x) % 2) * 4 + ((my + y) % 2) * 2 + (mc + c) % 2 for x, y, c in PEERS]

    def kcopy(b):
        return pltpu.make_async_copy(k_hbm.at[b], kbuf.at[b % SLOTS], ksem.at[b % SLOTS])

    def vcopy(b):
        return pltpu.make_async_copy(v_hbm.at[b], vbuf.at[b % SLOTS], vsem.at[b % SLOTS])

    qcopy = pltpu.make_async_copy(q_hbm, q_ref, qsem)
    qcopy.start()
    for b in range(SLOTS):
        kcopy(b).start()
        if b:
            vcopy(b - 1).start()
    vcopy(SLOTS - 1).start()

    barrier = pltpu.get_barrier_semaphore()
    for device in devices:
        pl.semaphore_signal(barrier, inc=1, device_id={"sp": device}, device_id_type=MESH)

    lane = lax.broadcasted_iota(jnp.int32, (GROUP, 2 * head), 1)
    row = lax.broadcasted_iota(jnp.int32, (GROUP, 2 * head), 0)
    own = [row == 2 * j + lane // head for j in range(GROUP // 2)]
    first = lane < head

    def scores(b, stat_tile):
        kcopy(b).wait()
        queries = q_ref[b].astype(jnp.float32)
        for g in range(groups):
            query = queries[g * GROUP : (g + 1) * GROUP]
            query = jnp.concatenate([query, query], 1)
            spread = jnp.concatenate([jnp.where(o, query, 0.0) for o in own], 1).astype(jnp.bfloat16)
            keys = kbuf[b % SLOTS, g * GROUP * head : (g + 1) * GROUP * head, :]
            s = jnp.dot(spread, keys, preferred_element_type=jnp.float32) * head**-0.5
            high = jnp.max(s, 1, keepdims=True)
            w = jnp.exp(s - high)
            weights[b % 2, g * GROUP : (g + 1) * GROUP, :] = w
            total = jnp.sum(w, 1, keepdims=True)
            at = g * 4 + (b % 2) * 2
            stat_tile = jnp.where(lane == at, high, jnp.where(lane == at + 1, total, stat_tile))
        return stat_tile

    def values(b):
        vcopy(b).wait()
        tiles = []
        for g in range(groups):
            w = weights[b % 2, g * GROUP : (g + 1) * GROUP, :].astype(jnp.bfloat16)
            block = vbuf[b % SLOTS, g * GROUP * head : (g + 1) * GROUP * head, :]
            seen = lax.dot_general(w, block, (((1,), (1,)), ((), ())), preferred_element_type=jnp.float32)
            folded = sum(jnp.where(o, seen[:, j * lanes : (j + 1) * lanes], 0.0) for j, o in enumerate(own))
            tiles.append(folded + pltpu.roll(folded, head, 1))
        return tiles

    def copies(p, kind):
        src, dst = ((part, parts), (stat, stats))[kind]
        return [
            pltpu.make_async_remote_copy(
                src_ref=src.at[p],
                dst_ref=dst.at[r, p],
                send_sem=send.at[p % 2, r, kind],
                recv_sem=recv.at[p, r, kind],
                device_id={"sp": device},
                device_id_type=MESH,
            )
            for r, device in enumerate(devices)
        ]

    def together(p):
        for copy in copies(p, 0) + copies(p, 1):
            copy.wait_recv()
        each = [stat[p]] + [stats[r, p] for r in range(len(PEERS))]
        high = functools.reduce(jnp.maximum, each)
        scale = [jnp.exp(e - high) for e in each]
        total = sum(pltpu.roll(e, 2 * head - 1, 1) * s for e, s in zip(each, scale))
        scale = [s / total for s in scale]
        result = [[], []]
        for h in range(groups // 2):
            tiles = [part[p, h * 2 * GROUP : (h + 1) * 2 * GROUP, :]] + [parts[r, p, h * 2 * GROUP : (h + 1) * 2 * GROUP, :] for r in range(len(PEERS))]
            tiles = [t.astype(jnp.float32) for t in tiles]
            both = []
            for i in range(2):
                g = 2 * h + i
                both.append(
                    sum(
                        t[i * GROUP : (i + 1) * GROUP] * jnp.where(first, s[:, 4 * g : 4 * g + 1], s[:, 4 * g + 2 : 4 * g + 3])
                        for t, s in zip(tiles, scale)
                    )
                )
            both = jnp.concatenate(both, 0)
            result[0].append(both[:, :head])
            result[1].append(pltpu.roll(both, head, 1)[:, :head])
        for i in range(2):
            out_ref[2 * p + i] = jnp.concatenate(result[i], 0).astype(out_ref.dtype)

    def refill(copy, b):
        @pl.when(b + SLOTS < batch)
        def _():
            copy(b + SLOTS).start()

    qcopy.wait()
    stat[0] = scores(0, jnp.zeros((GROUP, lanes), jnp.float32))
    refill(kcopy, 0)

    def pair(p, last):
        b = 2 * p
        even = values(b)
        stat[p] = scores(b + 1, stat[p])
        refill(vcopy, b)
        refill(kcopy, b + 1)
        if last:
            for copy in copies(p, 1):
                copy.start()
        odd = values(b + 1)
        for h in range(groups // 2):
            tile = jnp.concatenate([jnp.where(first, even[g], odd[g]) for g in (2 * h, 2 * h + 1)], 0)
            part[p, h * 2 * GROUP : (h + 1) * 2 * GROUP, :] = tile.astype(part.dtype)
        if last:
            for copy in copies(p, 0):
                copy.start()
        else:
            stat[p + 1] = scores(b + 2, jnp.zeros((GROUP, lanes), jnp.float32))
            refill(vcopy, b + 1)
            refill(kcopy, b + 2)

    def send_pair(p):
        for copy in copies(p, 0) + copies(p, 1):
            copy.start()

    def sent(p):
        for copy in copies(p, 0) + copies(p, 1):
            copy.wait_send()

    pair(0, False)
    pl.semaphore_wait(barrier, len(PEERS))

    @pl.loop(1, pairs - 1)
    def _(p):
        @pl.when(p >= 3)
        def _():
            sent(p - 3)

        send_pair(p - 1)
        pair(p, False)

        @pl.when(p >= LAG)
        def _():
            together(p - LAG)

    p = pairs - 1
    sent(p - 3)
    send_pair(p - 1)
    sent(p - 2)
    pair(p, True)

    @pl.loop(p - LAG, pairs)
    def _(c):
        together(c)

    sent(p - 1)
    sent(p)


def solution(mesh):
    def step(q, k, v):
        batch, tokens, heads, head = k.shape
        pairs = batch // 2
        k, v = (jnp.transpose(x, (0, 2, 3, 1)).reshape(batch, heads * head, tokens) for x in (k, v))
        n = len(PEERS)
        block = pltpu.VMEM((SLOTS, heads * head, tokens), jnp.bfloat16)
        return pl.pallas_call(
            functools.partial(attend, pairs, heads, head),
            out_shape=jax.ShapeDtypeStruct(q.shape, q.dtype),
            in_specs=[pl.BlockSpec(memory_space=pl.ANY)] * 3,
            out_specs=pl.BlockSpec(memory_space=pltpu.VMEM),
            scratch_shapes=[
                pltpu.VMEM(q.shape, q.dtype),
                block,
                block,
                pltpu.VMEM((2, heads, tokens), jnp.float32),
                pltpu.VMEM((pairs, heads, 2 * head), jnp.bfloat16),
                pltpu.VMEM((pairs, GROUP, 2 * head), jnp.float32),
                pltpu.VMEM((n, pairs, heads, 2 * head), jnp.bfloat16),
                pltpu.VMEM((n, pairs, GROUP, 2 * head), jnp.float32),
                pltpu.SemaphoreType.DMA,
                pltpu.SemaphoreType.DMA((SLOTS,)),
                pltpu.SemaphoreType.DMA((SLOTS,)),
                pltpu.SemaphoreType.DMA((2, n, 2)),
                pltpu.SemaphoreType.DMA((pairs, n, 2)),
            ],
            compiler_params=pltpu.CompilerParams(collective_id=0, has_side_effects=True, vmem_limit_bytes=48 * 2**20),
        )(q, k, v)

    return jax.shard_map(
        step,
        mesh=mesh,
        in_specs=(P("dp", None, None), P("dp", "sp", None, None), P("dp", "sp", None, None)),
        out_specs=P("dp", None, None),
        check_vma=False,
    )
```

time: 114 us -> 60 us (0.53)
  Pallas kernels: 0 us -> 58.2 us
  matrix products: 48.3 us -> 0 us
  waiting for transfers between devices: 33.7 us -> 0 us
  between operations: 13.4 us -> 0.01 us
  other arithmetic: 8.72 us -> 0 us
  local copies, waits for them, and re-layouts: 9.44 us -> 1.65 us
    pallas_call x0 -> x1, Pallas kernels: none -> 58.2 us  [step(): pl.pallas_call(functools.partial(attend, pairs, heads, head), out_shape=j...]
    dot_general x2 -> x0, matrix products: 48.3 us -> none  [einsum(): return jnp.einsum(form, a.astype(jnp.float32), b.astype(jnp.float32))]
    all_gather x1 -> x0, waiting for transfers between devices: 33.7 us -> none  [step(): return together(lax.all_gather(part_of(q, k, v), 'sp')).reshape(q.shape)]
    all_gather x1 -> x0, local copies, waits for them, and re-layouts: 7.62 us -> none  [step(): return together(lax.all_gather(part_of(q, k, v), 'sp')).reshape(q.shape)]
    reduce_sum x2 -> x0, other arithmetic: 5.69 us -> none  [the longest x1 4.69 us: together(): jnp.sum(seen * scale, 0) / jnp.sum(total * scale, 0)]
    unnamed x0 -> x3, local copies, waits for them, and re-layouts: none -> 1.65 us
    convert_element_type x1 -> x0, local copies, waits for them, and re-layouts: 1.27 us -> none  [together(): (jnp.sum(seen * scale, 0) / jnp.sum(total * scale, 0)).astype(jnp.bfloat16)]
    concatenate x1 -> x0, other arithmetic: 1.18 us -> none  [part_of(): jnp.concatenate([seen, jnp.sum(weights, -1, keepdims=True), high], -1)]
  transfers between devices with their start and end apart: 1 -> 0, of which waited for: 1 -> 0; matrix products, arithmetic and copies ran while one was open for 0% -> 0% of each run, Pallas kernels for 0% -> 0%
where the time goes in v1:
time: 60 us; the launch traced here: 59.8 us
  Pallas kernels  58.2 us (97%)
  local copies, waits for them, and re-layouts  1.65 us (3%)
    pallas_call x1, Pallas kernels, step(): pl.pallas_call(functools.partial(attend, pairs, heads, head), out_shape=j...  58.2 us
    unnamed x3, local copies, waits for them, and re-layouts  1.65 us

profile of v1, /device:TPU:0, one launch (start us, length us, event | category | flops | bytes accessed | tf_op | source)
XLA Modules:
  0.0 59.8 jit_solution(11630399972576174488)
XLA Ops:
  0.0 0.0 copy-start
  0.0 0.9 %copy-done = bf16[32,32,64]{2,1,0:T(8,128)(2,1)S(1)} copy-done((bf16[32,32,64]{2,1,0:T(8,128)(2,1)S(1)}, bf16[32,32,64]{2,1,0:T(8,128)(2,1)}, u32[]{:S(2)}) %copy-start) | copy-done | bytes 131096
  1.0 58.2 %shard_map.37 = bf16[32,32,64]{2,1,0:T(8,128)(2,1)S(1)} custom-call(bf16[32,32,64]{2,1,0:T(8,128)(2,1)S(1)} %copy-done, bf16[32,2048,512]{2,1,0:T(8,128)(2,1)} %bitcast.1.k_hbm, bf16[32,2048,512]{2,1,0:T(8,128)(2,1)} %bitcast.3.v_hbm), custom_call_target="tpu_custom_call" | custom-call | tf_op jit(solution)/shard_map/pallas_call | solution.py:191
  59.1 0.7 %copy.5 = bf16[32,32,64]{2,1,0:T(8,128)(2,1)} copy(bf16[32,32,64]{2,1,0:T(8,128)(2,1)S(1)} %shard_map.37) | data formatting | bytes 262144
Async XLA Ops:
  0.0 0.9 %copy-start = (bf16[32,32,64]{2,1,0:T(8,128)(2,1)S(1)}, bf16[32,32,64]{2,1,0:T(8,128)(2,1)}, u32[]{:S(2)}) copy-start(bf16[32,32,64]{2,1,0:T(8,128)(2,1)} %q_hbm.1) | copy-start | bytes 393220

commit v2 on v1

v2 whole, which is shorter than its diff:
```python
import functools

import jax
import jax.numpy as jnp
from jax import lax
from jax.experimental import pallas as pl
from jax.experimental.pallas import tpu as pltpu
from jax.sharding import PartitionSpec as P

MESH = pl.DeviceIdType.MESH
SLOTS = 6
LAG = 4
GROUP = 8
PEERS = [(x, y, c) for x in (1, 0) for y in (1, 0) for c in (1, 0)][:-1]


def add(terms):
    return functools.reduce(jnp.add, terms)


def attend(pairs, heads, head, q_hbm, k_hbm, v_hbm, out_ref, q_ref, kbuf, vbuf, weights, part, stat, parts, stats, qsem, ksem, vsem, lsem, send, recv):
    batch, groups, lanes = 2 * pairs, heads // GROUP, 2 * head
    rows = GROUP * head
    me = lax.axis_index("sp")
    mx, my, mc = me // 4, (me // 2) % 2, me % 2
    devices = [((mx + x) % 2) * 4 + ((my + y) % 2) * 2 + (mc + c) % 2 for x, y, c in PEERS]

    def kcopy(b):
        return pltpu.make_async_copy(k_hbm.at[b], kbuf.at[b % SLOTS], ksem.at[b % SLOTS])

    def vcopy(b):
        return pltpu.make_async_copy(v_hbm.at[b], vbuf.at[b % SLOTS], vsem.at[b % SLOTS])

    def vpiece(b, g):
        piece = pl.ds(g * rows, rows)
        return pltpu.make_async_copy(v_hbm.at[b, piece], vbuf.at[b % SLOTS, piece], lsem.at[b % 2, g])

    qcopy = pltpu.make_async_copy(q_hbm, q_ref, qsem)
    qcopy.start()
    kcopy(0).start()
    kcopy(1).start()
    for b in range(SLOTS - 2):
        kcopy(b + 2).start()
        vcopy(b).start()

    barrier = pltpu.get_barrier_semaphore()
    for device in devices:
        pl.semaphore_signal(barrier, inc=1, device_id={"sp": device}, device_id_type=MESH)

    lane = lax.broadcasted_iota(jnp.int32, (GROUP, lanes), 1)
    row = lax.broadcasted_iota(jnp.int32, (GROUP, lanes), 0)
    own = [row == 2 * j + lane // head for j in range(GROUP // 2)]
    odd = (lane // head) == row % 2

    def scores(b, i, stat_tile):
        queries = q_ref[b].astype(jnp.float32)
        for g in range(groups):
            query = queries[g * GROUP : (g + 1) * GROUP]
            query = jnp.concatenate([query, query], 1)
            spread = jnp.concatenate([jnp.where(o, query, 0.0) for o in own], 1).astype(jnp.bfloat16)
            keys = kbuf[b % SLOTS, g * rows : (g + 1) * rows, :]
            s = jnp.dot(spread, keys, preferred_element_type=jnp.float32) * head**-0.5
            high = jnp.max(s, 1, keepdims=True)
            w = jnp.exp(s - high)
            weights[i, g * GROUP : (g + 1) * GROUP, :] = w
            total = jnp.sum(w, 1, keepdims=True)
            at = g * 4 + i * 2
            stat_tile = jnp.where(lane == at, high, jnp.where(lane == at + 1, total, stat_tile))
        return stat_tile

    def values(b, i, g):
        w = weights[i, g * GROUP : (g + 1) * GROUP, :].astype(jnp.bfloat16)
        block = vbuf[b % SLOTS, g * rows : (g + 1) * rows, :]
        seen = lax.dot_general(w, block, (((1,), (1,)), ((), ())), preferred_element_type=jnp.float32)
        return add(jnp.where(o, seen[:, j * lanes : (j + 1) * lanes], 0.0) for j, o in enumerate(own))

    def stat_copies(p):
        return [
            pltpu.make_async_remote_copy(
                src_ref=stat.at[p],
                dst_ref=stats.at[r, p],
                send_sem=send.at[p % 2, r, 0],
                recv_sem=recv.at[p, r, 0],
                device_id={"sp": device},
                device_id_type=MESH,
            )
            for r, device in enumerate(devices)
        ]

    def part_copies(p, at=0, size=heads, sem=1):
        piece = pl.ds(at, size)
        return [
            pltpu.make_async_remote_copy(
                src_ref=part.at[p, piece],
                dst_ref=parts.at[r, p, piece],
                send_sem=send.at[p % 2, r, sem],
                recv_sem=recv.at[p, r, sem],
                device_id={"sp": device},
                device_id_type=MESH,
            )
            for r, device in enumerate(devices)
        ]

    def half_copies(p, h):
        return part_copies(p, h * 2 * GROUP, 2 * GROUP, 1 + h)

    def scales(p):
        each = [stat[p]] + [stats[r, p] for r in range(len(PEERS))]
        high = functools.reduce(jnp.maximum, each)
        scale = [jnp.exp(e - high) for e in each]
        total = add(pltpu.roll(e, lanes - 1, 1) * s for e, s in zip(each, scale))
        scale = [s / total for s in scale]
        return [[jnp.where(odd, s[:, 4 * g + 2 : 4 * g + 3], s[:, 4 * g : 4 * g + 1]) for s in scale] for g in range(groups)]

    def together(p, h, scale):
        piece = slice(h * 2 * GROUP, (h + 1) * 2 * GROUP)
        tiles = [t.astype(jnp.float32) for t in [part[p, piece, :]] + [parts[r, p, piece, :] for r in range(len(PEERS))]]
        result = [[], []]
        for i in range(2):
            both = add(t[i * GROUP : (i + 1) * GROUP] * s for t, s in zip(tiles, scale[2 * h + i]))
            swapped = pltpu.roll(both, head, 1)
            result[0].append(jnp.where(row % 2 == 0, swapped, both)[:, :head])
            result[1].append(jnp.where(row % 2 == 0, both, swapped)[:, :head])
        for i in range(2):
            out_ref[2 * p + i, piece, :] = jnp.concatenate(result[i], 0).astype(out_ref.dtype)

    def store(p, even, odd_tiles, h):
        tile = jnp.concatenate([pltpu.roll(even[g], head, 1) + odd_tiles[g] for g in (2 * h, 2 * h + 1)], 0)
        part[p, h * 2 * GROUP : (h + 1) * 2 * GROUP, :] = tile.astype(part.dtype)

    def pair(p, combine, last=False):
        b = 2 * p
        tiles = [None, None]
        stat_tile = jnp.zeros((GROUP, lanes), jnp.float32)
        for i in range(2):
            vcopy(b + i).wait()
            kcopy(b + i + 2).wait()
            if combine and i == 0:
                for copy in stat_copies(p - LAG) + part_copies(p - LAG):
                    copy.wait_recv()
            tiles[i] = [values(b + i, i, g) for g in range(groups)]
            stat_tile = scores(b + i + 2, i, stat_tile)
            if combine:
                if i == 0:
                    scale = scales(p - LAG)
                together(p - LAG, i, scale)
            if i:
                stat[p + 1] = stat_tile
                for h in range(groups // 2):
                    store(p, *tiles, h)

            @pl.when(b + i + SLOTS < batch - 2)
            def _():
                vcopy(b + i + SLOTS).start()

            for g in range(groups):

                @pl.when(jnp.logical_and(b + i + SLOTS >= batch - 2, b + i + SLOTS < batch))
                def _():
                    vpiece(b + i + SLOTS, g).start()

            @pl.when(b + i + 2 + SLOTS < batch)
            def _():
                kcopy(b + i + 2 + SLOTS).start()

    def send_pair(p):
        for copy in stat_copies(p) + part_copies(p):
            copy.start()

    def sent(p):
        for copy in stat_copies(p) + part_copies(p):
            copy.wait_send()

    qcopy.wait()
    stat_tile = jnp.zeros((GROUP, lanes), jnp.float32)
    for b in range(2):
        kcopy(b).wait()
        stat_tile = scores(b, b, stat_tile)
        kcopy(b + SLOTS).start()
        vcopy(b + SLOTS - 2).start()
    stat[0] = stat_tile

    pair(0, False)
    pl.semaphore_wait(barrier, len(PEERS))

    def step(p, combine):
        @pl.when(p >= 3)
        def _():
            sent(p - 3)

        send_pair(p - 1)
        pair(p, combine)

    @pl.loop(1, LAG)
    def _(p):
        step(p, False)

    @pl.loop(LAG, pairs - 1)
    def _(p):
        step(p, True)

    p = pairs - 1
    sent(p - 3)
    send_pair(p - 1)
    sent(p - 2)
    for copy in stat_copies(p):
        copy.start()
    even = []
    for g in range(groups):
        vpiece(batch - 2, g).wait()
        even.append(values(batch - 2, 0, g))
    for h in range(groups // 2):
        odd_tiles = {}
        for g in (2 * h, 2 * h + 1):
            vpiece(batch - 1, g).wait()
            odd_tiles[g] = values(batch - 1, 1, g)
        store(p, even, odd_tiles, h)
        for copy in half_copies(p, h):
            copy.start()

    @pl.loop(p - LAG, p)
    def _(c):
        for copy in stat_copies(c) + part_copies(c):
            copy.wait_recv()
        scale = scales(c)
        for h in range(groups // 2):
            together(c, h, scale)

    for copy in stat_copies(p):
        copy.wait_recv()
    scale = scales(p)
    for h in range(groups // 2):
        for copy in half_copies(p, h):
            copy.wait_recv()
        together(p, h, scale)

    sent(p - 1)
    for copy in stat_copies(p) + half_copies(p, 0) + half_copies(p, 1):
        copy.wait_send()


def solution(mesh):
    def step(q, k, v):
        batch, tokens, heads, head = k.shape
        pairs = batch // 2
        k, v = (jnp.transpose(x, (0, 2, 3, 1)).reshape(batch, heads * head, tokens) for x in (k, v))
        q = pltpu.with_memory_space_constraint(q, pltpu.HBM)
        n, groups = len(PEERS), heads // GROUP
        block = pltpu.VMEM((SLOTS, heads * head, tokens), jnp.bfloat16)
        return pl.pallas_call(
            functools.partial(attend, pairs, heads, head),
            out_shape=jax.ShapeDtypeStruct(q.shape, q.dtype),
            in_specs=[pl.BlockSpec(memory_space=pltpu.HBM)] * 3,
            out_specs=pl.BlockSpec(memory_space=pltpu.VMEM),
            scratch_shapes=[
                pltpu.VMEM(q.shape, q.dtype),
                block,
                block,
                pltpu.VMEM((2, heads, tokens), jnp.float32),
                pltpu.VMEM((pairs, heads, 2 * head), jnp.bfloat16),
                pltpu.VMEM((pairs, GROUP, 2 * head), jnp.float32),
                pltpu.VMEM((n, pairs, heads, 2 * head), jnp.bfloat16),
                pltpu.VMEM((n, pairs, GROUP, 2 * head), jnp.float32),
                pltpu.SemaphoreType.DMA,
                pltpu.SemaphoreType.DMA((SLOTS,)),
                pltpu.SemaphoreType.DMA((SLOTS,)),
                pltpu.SemaphoreType.DMA((2, groups)),
                pltpu.SemaphoreType.DMA((2, n, 3)),
                pltpu.SemaphoreType.DMA((pairs, n, 3)),
            ],
            compiler_params=pltpu.CompilerParams(collective_id=0, has_side_effects=True, vmem_limit_bytes=48 * 2**20),
        )(q, k, v)

    return jax.shard_map(
        step,
        mesh=mesh,
        in_specs=(P("dp", None, None), P("dp", "sp", None, None), P("dp", "sp", None, None)),
        out_specs=P("dp", None, None),
        check_vma=False,
    )
```

time: 60 us -> 54.5 us (0.908)
  Pallas kernels: 58.2 us -> 53.7 us
  local copies, waits for them, and re-layouts: 1.65 us -> 0.71 us
    pallas_call x1, Pallas kernels: 58.2 us -> 53.7 us  [step(): pl.pallas_call(functools.partial(attend, pairs, heads, head), out_shape=j...]
    unnamed x3 -> x1, local copies, waits for them, and re-layouts: 1.65 us -> 0.71 us
where the time goes in v2:
time: 54.5 us; the launch traced here: 54.4 us
  Pallas kernels  53.7 us (99%)
  local copies, waits for them, and re-layouts  0.71 us (1%)
    pallas_call x1, Pallas kernels, step(): pl.pallas_call(functools.partial(attend, pairs, heads, head), out_shape=j...  53.7 us

profile of v2, /device:TPU:0, one launch (start us, length us, event | category | flops | bytes accessed | tf_op | source)
XLA Modules:
  0.0 54.4 jit_solution(10875668796792763600)
XLA Ops:
  0.0 53.7 %shard_map.37 = bf16[32,32,64]{2,1,0:T(8,128)(2,1)S(1)} custom-call(bf16[32,32,64]{2,1,0:T(8,128)(2,1)} %q_hbm.1, bf16[32,2048,512]{2,1,0:T(8,128)(2,1)} %bitcast.1.k_hbm, bf16[32,2048,512]{2,1,0:T(8,128)(2,1)} %bitcast.3.v_hbm), custom_call_target="tpu_custom_call" | custom-call | tf_op jit(solution)/shard_map/pallas_call | solution.py:250
  53.7 0.7 %copy.5 = bf16[32,32,64]{2,1,0:T(8,128)(2,1)} copy(bf16[32,32,64]{2,1,0:T(8,128)(2,1)S(1)} %shard_map.37) | data formatting | bytes 262144

commit v3 on v2

v3 whole, which is shorter than its diff:
```python
import functools

import jax
import jax.numpy as jnp
from jax import lax
from jax.experimental import pallas as pl
from jax.experimental.pallas import tpu as pltpu
from jax.sharding import PartitionSpec as P

MESH = pl.DeviceIdType.MESH
SLOTS = 6
LAG = 4
RING = 2 * LAG + 1
GROUP = 8
PEERS = [(x, y, c) for x in (1, 0) for y in (1, 0) for c in (1, 0)][:-1]


def add(terms):
    return functools.reduce(jnp.add, terms)


def attend(pairs, heads, head, q_hbm, k_hbm, v_hbm, out_ref, q_ref, kbuf, vbuf, raw, weights, part, stat, parts, stats, qsem, ksem, vsem, lsem, send, recv):
    batch, groups, lanes = 2 * pairs, heads // GROUP, 2 * head
    rows = GROUP * head
    me = lax.axis_index("sp")
    mx, my, mc = me // 4, (me // 2) % 2, me % 2
    devices = [((mx + x) % 2) * 4 + ((my + y) % 2) * 2 + (mc + c) % 2 for x, y, c in PEERS]

    def kcopy(b):
        return pltpu.make_async_copy(k_hbm.at[b], kbuf.at[b % SLOTS], ksem.at[b % SLOTS])

    def vcopy(b):
        return pltpu.make_async_copy(v_hbm.at[b], vbuf.at[b % SLOTS], vsem.at[b % SLOTS])

    def vpiece(b, g):
        piece = pl.ds(g * rows, rows)
        return pltpu.make_async_copy(v_hbm.at[b, piece], vbuf.at[b % SLOTS, piece], lsem.at[b % 2, g])

    qcopy = pltpu.make_async_copy(q_hbm, q_ref, qsem)
    qcopy.start()
    for b in range(4):
        kcopy(b).start(priority=1)
    for b in range(SLOTS - 2):
        vcopy(b).start(priority=1)
        if b + 4 < SLOTS:
            kcopy(b + 4).start(priority=1)

    barrier = pltpu.get_barrier_semaphore()
    for device in devices:
        pl.semaphore_signal(barrier, inc=1, device_id={"sp": device}, device_id_type=MESH)

    lane = lax.broadcasted_iota(jnp.int32, (GROUP, lanes), 1)
    row = lax.broadcasted_iota(jnp.int32, (GROUP, lanes), 0)
    own = [row == 2 * j + lane // head for j in range(GROUP // 2)]
    odd = (lane // head) == row % 2

    def score(b, i, g):
        query = q_ref[b, g * GROUP : (g + 1) * GROUP, :].astype(jnp.float32)
        query = jnp.concatenate([query, query], 1)
        spread = jnp.concatenate([jnp.where(o, query, 0.0) for o in own], 1).astype(jnp.bfloat16)
        keys = kbuf[b % SLOTS, g * rows : (g + 1) * rows, :]
        raw[i, g * GROUP : (g + 1) * GROUP, :] = jnp.dot(spread, keys, preferred_element_type=jnp.float32)

    def soften():
        stat_tile = jnp.zeros((GROUP, lanes), jnp.float32)
        for i in range(2):
            for g in range(groups):
                s = raw[i, g * GROUP : (g + 1) * GROUP, :] * head**-0.5
                high = jnp.max(s, 1, keepdims=True)
                w = jnp.exp(s - high)
                weights[i, g * GROUP : (g + 1) * GROUP, :] = w.astype(weights.dtype)
                total = jnp.sum(w, 1, keepdims=True)
                at = g * 4 + i * 2
                stat_tile = jnp.where(lane == at, high, jnp.where(lane == at + 1, total, stat_tile))
        return stat_tile

    def values(b, i, g):
        w = weights[i, g * GROUP : (g + 1) * GROUP, :].astype(jnp.bfloat16)
        block = vbuf[b % SLOTS, g * rows : (g + 1) * rows, :]
        seen = lax.dot_general(w, block, (((1,), (1,)), ((), ())), preferred_element_type=jnp.float32)
        return add(jnp.where(o, seen[:, j * lanes : (j + 1) * lanes], 0.0) for j, o in enumerate(own))

    def copies(src, dst, kind, p):
        return [
            pltpu.make_async_remote_copy(
                src_ref=src,
                dst_ref=dst.at[r],
                send_sem=send.at[kind, p % 2],
                recv_sem=recv.at[kind, p % RING],
                device_id={"sp": device},
                device_id_type=MESH,
            )
            for r, device in enumerate(devices)
        ]

    def arrived(dst, kind, p):
        return pltpu.make_async_remote_copy(
            src_ref=dst,
            dst_ref=dst,
            send_sem=send.at[kind, p % 2],
            recv_sem=recv.at[kind, p % RING],
            device_id={"sp": devices[0]},
            device_id_type=MESH,
        )

    def half(h):
        return pl.ds(h * 2 * GROUP, 2 * GROUP)

    def send_stat(p):
        for copy in copies(stat.at[p], stats.at[:, p], 0, p):
            copy.start()

    def send_part(p):
        for copy in copies(part.at[p], parts.at[:, p], 1, p):
            copy.start()

    def send_half(p, h):
        for copy in copies(part.at[p, half(h)], parts.at[:, p, half(h)], 1 + h, p):
            copy.start()

    def scales(p):
        each = [stat[p]] + [stats[r, p] for r in range(len(PEERS))]
        high = functools.reduce(jnp.maximum, each)
        scale = [jnp.exp(e - high) for e in each]
        total = add(pltpu.roll(e, lanes - 1, 1) * s for e, s in zip(each, scale))
        scale = [s / total for s in scale]
        return [[jnp.where(odd, s[:, 4 * g + 2 : 4 * g + 3], s[:, 4 * g : 4 * g + 1]) for s in scale] for g in range(groups)]

    def together(p, h, scale):
        piece = slice(h * 2 * GROUP, (h + 1) * 2 * GROUP)
        tiles = [t.astype(jnp.float32) for t in [part[p, piece, :]] + [parts[r, p, piece, :] for r in range(len(PEERS))]]
        result = [[], []]
        for i in range(2):
            both = add(t[i * GROUP : (i + 1) * GROUP] * s for t, s in zip(tiles, scale[2 * h + i]))
            swapped = pltpu.roll(both, head, 1)
            result[0].append(jnp.where(row % 2 == 0, swapped, both)[:, :head])
            result[1].append(jnp.where(row % 2 == 0, both, swapped)[:, :head])
        for i in range(2):
            out_ref[2 * p + i, piece, :] = jnp.concatenate(result[i], 0).astype(out_ref.dtype)

    def store(p, even, odd_tiles, h):
        tile = jnp.concatenate([pltpu.roll(even[g], head, 1) + odd_tiles[g] for g in (2 * h, 2 * h + 1)], 0)
        part[p, h * 2 * GROUP : (h + 1) * 2 * GROUP, :] = tile.astype(part.dtype)

    def attended(p):
        return [[values(2 * p + i, i, g) for g in range(groups)] for i in range(2)]

    def pair(p, combine):
        b = 2 * p
        for i in range(2):
            vcopy(b + i).wait()
            kcopy(b + i + 4).wait()
        if combine:
            received(p - LAG)
        tiles = attended(p)
        stat[p + 1] = soften()
        for i in range(2):
            for g in range(groups):
                score(b + i + 4, i, g)
        if combine:
            scale = scales(p - LAG)
            for h in range(groups // 2):
                together(p - LAG, h, scale)
        for h in range(groups // 2):
            store(p, *tiles, h)
        refill(b)

    def refill(b):
        for i in range(2):
            v, k = b + i + SLOTS, b + i + 4 + SLOTS

            @pl.when(v < batch - 2)
            def _():
                vcopy(v).start(priority=1)

            @pl.when(jnp.logical_and(v >= batch - 2, v < batch))
            def _():
                for g in range(groups):
                    vpiece(v, g).start(priority=1)

            @pl.when(k < batch)
            def _():
                kcopy(k).start(priority=1)

    def received(p):
        arrived(stats.at[:, p], 0, p).wait_recv()
        arrived(parts.at[:, p], 1, p).wait_recv()

    def send_pair(p):
        send_stat(p)
        send_part(p)

    def sent(p):
        arrived(stats.at[:, p], 0, p).wait_send()
        arrived(parts.at[:, p], 1, p).wait_send()

    qcopy.wait()
    for i in range(2):
        kcopy(i).wait()
    for i in range(2):
        for g in range(groups):
            score(i, i, g)
    for i in range(2):
        kcopy(i + SLOTS).start(priority=1)
        kcopy(i + 2).wait()
    stat[0] = soften()
    for i in range(2):
        for g in range(groups):
            score(i + 2, i, g)
    for i in range(2):
        kcopy(i + 2 + SLOTS).start(priority=1)
        vcopy(i + SLOTS - 2).start(priority=1)

    pair(0, False)
    pl.semaphore_wait(barrier, len(PEERS))

    def step(p, combine):
        @pl.when(p >= 3)
        def _():
            sent(p - 3)

        send_pair(p - 1)
        pair(p, combine)

    @pl.loop(1, LAG)
    def _(p):
        step(p, False)

    @pl.loop(LAG, pairs - 2)
    def _(p):
        step(p, True)

    p = pairs - 2
    sent(p - 3)
    send_pair(p - 1)
    for i in range(2):
        vcopy(2 * p + i).wait()
    received(p - LAG)
    tiles = attended(p)
    stat[p + 1] = soften()
    scale = scales(p - LAG)
    for h in range(groups // 2):
        together(p - LAG, h, scale)
        store(p, *tiles, h)

    p = pairs - 1
    sent(p - 3)
    send_pair(p - 1)
    sent(p - 2)
    send_stat(p)
    even = []
    for g in range(groups):
        vpiece(batch - 2, g).wait()
        even.append(values(batch - 2, 0, g))
    for h in range(groups // 2):
        odd_tiles = {}
        for g in (2 * h, 2 * h + 1):
            vpiece(batch - 1, g).wait()
            odd_tiles[g] = values(batch - 1, 1, g)
        store(p, even, odd_tiles, h)
        send_half(p, h)

    @pl.loop(p - LAG, p)
    def _(c):
        received(c)
        scale = scales(c)
        for h in range(groups // 2):
            together(c, h, scale)

    arrived(stats.at[:, p], 0, p).wait_recv()
    scale = scales(p)
    for h in range(groups // 2):
        arrived(parts.at[:, p, half(h)], 1 + h, p).wait_recv()
        together(p, h, scale)

    sent(p - 1)
    arrived(stats.at[:, p], 0, p).wait_send()
    for h in range(groups // 2):
        arrived(parts.at[:, p, half(h)], 1 + h, p).wait_send()


def solution(mesh):
    def step(q, k, v):
        batch, tokens, heads, head = k.shape
        pairs = batch // 2
        k, v = (jnp.transpose(x, (0, 2, 3, 1)).reshape(batch, heads * head, tokens) for x in (k, v))
        q = pltpu.with_memory_space_constraint(q, pltpu.HBM)
        n, groups = len(PEERS), heads // GROUP
        block = pltpu.VMEM((SLOTS, heads * head, tokens), jnp.bfloat16)
        return pl.pallas_call(
            functools.partial(attend, pairs, heads, head),
            out_shape=jax.ShapeDtypeStruct(q.shape, q.dtype),
            in_specs=[pl.BlockSpec(memory_space=pltpu.HBM)] * 3,
            out_specs=pl.BlockSpec(memory_space=pltpu.VMEM),
            scratch_shapes=[
                pltpu.VMEM(q.shape, q.dtype),
                block,
                block,
                pltpu.VMEM((2, heads, tokens), jnp.float32),
                pltpu.VMEM((2, heads, tokens), jnp.float32),
                pltpu.VMEM((pairs, heads, 2 * head), jnp.bfloat16),
                pltpu.VMEM((pairs, GROUP, 2 * head), jnp.float32),
                pltpu.VMEM((n, pairs, heads, 2 * head), jnp.bfloat16),
                pltpu.VMEM((n, pairs, GROUP, 2 * head), jnp.float32),
                pltpu.SemaphoreType.DMA,
                pltpu.SemaphoreType.DMA((SLOTS,)),
                pltpu.SemaphoreType.DMA((SLOTS,)),
                pltpu.SemaphoreType.DMA((2, groups)),
                pltpu.SemaphoreType.DMA((3, 2)),
                pltpu.SemaphoreType.DMA((3, RING)),
            ],
            compiler_params=pltpu.CompilerParams(collective_id=0, has_side_effects=True, vmem_limit_bytes=48 * 2**20),
        )(q, k, v)

    return jax.shard_map(
        step,
        mesh=mesh,
        in_specs=(P("dp", None, None), P("dp", "sp", None, None), P("dp", "sp", None, None)),
        out_specs=P("dp", None, None),
        check_vma=False,
    )
```

time: 54.5 us -> 50.2 us (0.921)
  Pallas kernels: 53.7 us -> 49.4 us
    pallas_call x1, Pallas kernels: 53.7 us -> 49.4 us  [step(): pl.pallas_call(functools.partial(attend, pairs, heads, head), out_shape=j...]
where the time goes in v3:
time: 50.2 us; the launch traced here: 50.1 us
  Pallas kernels  49.4 us (98%)
  local copies, waits for them, and re-layouts  0.71 us (1%)
    pallas_call x1, Pallas kernels, step(): pl.pallas_call(functools.partial(attend, pairs, heads, head), out_shape=j...  49.4 us

profile of v3, /device:TPU:0, one launch (start us, length us, event | category | flops | bytes accessed | tf_op | source)
XLA Modules:
  0.0 50.1 jit_solution(4838532193519225497)
XLA Ops:
  0.0 49.4 %shard_map.37 = bf16[32,32,64]{2,1,0:T(8,128)(2,1)S(1)} custom-call(bf16[32,32,64]{2,1,0:T(8,128)(2,1)} %q_hbm.1, bf16[32,2048,512]{2,1,0:T(8,128)(2,1)} %bitcast.1.k_hbm, bf16[32,2048,512]{2,1,0:T(8,128)(2,1)} %bitcast.3.v_hbm), custom_call_target="tpu_custom_call" | custom-call | tf_op jit(solution)/shard_map/pallas_call | solution.py:290
  49.4 0.7 %copy.5 = bf16[32,32,64]{2,1,0:T(8,128)(2,1)} copy(bf16[32,32,64]{2,1,0:T(8,128)(2,1)S(1)} %shard_map.37) | data formatting | bytes 262144

commit v4 on v3

--- a/solution.py
+++ b/solution.py
@@ -9,7 +9,7 @@
 
 MESH = pl.DeviceIdType.MESH
 SLOTS = 6
-LAG = 4
+LAG = 3
 RING = 2 * LAG + 1
 GROUP = 8
 PEERS = [(x, y, c) for x in (1, 0) for y in (1, 0) for c in (1, 0)][:-1]
@@ -19,7 +19,7 @@
     return functools.reduce(jnp.add, terms)
 
 
-def attend(pairs, heads, head, q_hbm, k_hbm, v_hbm, out_ref, q_ref, kbuf, vbuf, raw, weights, part, stat, parts, stats, qsem, ksem, vsem, lsem, send, recv):
+def attend(pairs, heads, head, q_hbm, k_hbm, v_hbm, out_ref, q_ref, kbuf, vbuf, raw, weights, part, stat, parts, stats, qsem, ksem, vsem, send, recv):
     batch, groups, lanes = 2 * pairs, heads // GROUP, 2 * head
     rows = GROUP * head
     me = lax.axis_index("sp")
@@ -31,10 +31,6 @@
 
     def vcopy(b):
         return pltpu.make_async_copy(v_hbm.at[b], vbuf.at[b % SLOTS], vsem.at[b % SLOTS])
-
-    def vpiece(b, g):
-        piece = pl.ds(g * rows, rows)
-        return pltpu.make_async_copy(v_hbm.at[b, piece], vbuf.at[b % SLOTS, piece], lsem.at[b % 2, g])
 
     qcopy = pltpu.make_async_copy(q_hbm, q_ref, qsem)
     qcopy.start()
@@ -61,18 +57,18 @@
         keys = kbuf[b % SLOTS, g * rows : (g + 1) * rows, :]
         raw[i, g * GROUP : (g + 1) * GROUP, :] = jnp.dot(spread, keys, preferred_element_type=jnp.float32)
 
-    def soften():
-        stat_tile = jnp.zeros((GROUP, lanes), jnp.float32)
-        for i in range(2):
-            for g in range(groups):
-                s = raw[i, g * GROUP : (g + 1) * GROUP, :] * head**-0.5
-                high = jnp.max(s, 1, keepdims=True)
-                w = jnp.exp(s - high)
-                weights[i, g * GROUP : (g + 1) * GROUP, :] = w.astype(weights.dtype)
-                total = jnp.sum(w, 1, keepdims=True)
-                at = g * 4 + i * 2
-                stat_tile = jnp.where(lane == at, high, jnp.where(lane == at + 1, total, stat_tile))
+    def soften(i, stat_tile):
+        for g in range(groups):
+            s = raw[i, g * GROUP : (g + 1) * GROUP, :] * head**-0.5
+            high = jnp.max(s, 1, keepdims=True)
+            w = jnp.exp(s - high)
+            weights[i, g * GROUP : (g + 1) * GROUP, :] = w
+            total = jnp.sum(w, 1, keepdims=True)
+            at = g * 4 + i * 2
+            stat_tile = jnp.where(lane == at, high, jnp.where(lane == at + 1, total, stat_tile))
         return stat_tile
+
+    nothing = jnp.zeros((GROUP, lanes), jnp.float32)
 
     def values(b, i, g):
         w = weights[i, g * GROUP : (g + 1) * GROUP, :].astype(jnp.bfloat16)
@@ -85,8 +81,8 @@
             pltpu.make_async_remote_copy(
                 src_ref=src,
                 dst_ref=dst.at[r],
-                send_sem=send.at[kind, p % 2],
-                recv_sem=recv.at[kind, p % RING],
+                send_sem=send.at[kind * 2 + (p % 2 if kind < 2 else 0)],
+                recv_sem=recv.at[kind * RING + (p % RING if kind < 2 else 0)],
                 device_id={"sp": device},
                 device_id_type=MESH,
             )
@@ -97,8 +93,8 @@
         return pltpu.make_async_remote_copy(
             src_ref=dst,
             dst_ref=dst,
-            send_sem=send.at[kind, p % 2],
-            recv_sem=recv.at[kind, p % RING],
+            send_sem=send.at[kind * 2 + (p % 2 if kind < 2 else 0)],
+            recv_sem=recv.at[kind * RING + (p % RING if kind < 2 else 0)],
             device_id={"sp": devices[0]},
             device_id_type=MESH,
         )
@@ -142,8 +138,8 @@
         tile = jnp.concatenate([pltpu.roll(even[g], head, 1) + odd_tiles[g] for g in (2 * h, 2 * h + 1)], 0)
         part[p, h * 2 * GROUP : (h + 1) * 2 * GROUP, :] = tile.astype(part.dtype)
 
-    def attended(p):
-        return [[values(2 * p + i, i, g) for g in range(groups)] for i in range(2)]
+    def attended(b, i):
+        return [values(b, i, g) for g in range(groups)]
 
     def pair(p, combine):
         b = 2 * p
@@ -152,8 +148,8 @@
             kcopy(b + i + 4).wait()
         if combine:
             received(p - LAG)
-        tiles = attended(p)
-        stat[p + 1] = soften()
+        tiles = [attended(b + i, i) for i in range(2)]
+        stat[p + 1] = soften(1, soften(0, nothing))
         for i in range(2):
             for g in range(groups):
                 score(b + i + 4, i, g)
@@ -169,14 +165,9 @@
         for i in range(2):
             v, k = b + i + SLOTS, b + i + 4 + SLOTS
 
-            @pl.when(v < batch - 2)
+            @pl.when(v < batch)
             def _():
                 vcopy(v).start(priority=1)
-
-            @pl.when(jnp.logical_and(v >= batch - 2, v < batch))
-            def _():
-                for g in range(groups):
-                    vpiece(v, g).start(priority=1)
 
             @pl.when(k < batch)
             def _():
@@ -203,7 +194,7 @@
     for i in range(2):
         kcopy(i + SLOTS).start(priority=1)
         kcopy(i + 2).wait()
-    stat[0] = soften()
+    stat[0] = soften(1, soften(0, nothing))
     for i in range(2):
         for g in range(groups):
             score(i + 2, i, g)
@@ -226,46 +217,53 @@
     def _(p):
         step(p, False)
 
-    @pl.loop(LAG, pairs - 2)
+    @pl.loop(LAG, pairs - 3)
     def _(p):
         step(p, True)
 
-    p = pairs - 2
-    sent(p - 3)
-    send_pair(p - 1)
-    for i in range(2):
-        vcopy(2 * p + i).wait()
-    received(p - LAG)
-    tiles = attended(p)
-    stat[p + 1] = soften()
-    scale = scales(p - LAG)
-    for h in range(groups // 2):
-        together(p - LAG, h, scale)
-        store(p, *tiles, h)
+    for p in range(pairs - 3, pairs - 1):
+        sent(p - 3)
+        send_pair(p - 1)
+        received(p - LAG)
+        tiles, stat_tile = [], nothing
+        for i in range(2):
+            b = 2 * p + i
+            vcopy(b).wait()
+            if b + 4 < batch:
+                kcopy(b + 4).wait()
+            tiles.append(attended(b, i))
+            stat_tile = soften(i, stat_tile)
+            if b + 4 < batch:
+                for g in range(groups):
+                    score(b + 4, i, g)
+        stat[p + 1] = stat_tile
+        for h in range(groups // 2):
+            store(p, *tiles, h)
 
     p = pairs - 1
     sent(p - 3)
     send_pair(p - 1)
     sent(p - 2)
     send_stat(p)
-    even = []
-    for g in range(groups):
-        vpiece(batch - 2, g).wait()
-        even.append(values(batch - 2, 0, g))
+    vcopy(batch - 2).wait()
+    even = attended(batch - 2, 0)
+    vcopy(batch - 1).wait()
     for h in range(groups // 2):
-        odd_tiles = {}
-        for g in (2 * h, 2 * h + 1):
-            vpiece(batch - 1, g).wait()
-            odd_tiles[g] = values(batch - 1, 1, g)
+        odd_tiles = {g: values(batch - 1, 1, g) for g in (2 * h, 2 * h + 1)}
         store(p, even, odd_tiles, h)
         send_half(p, h)
+
+    def combine(c):
+        scale = scales(c)
+        for h in range(groups // 2):
+            together(c, h, scale)
+
+    pl.loop(p - 2 - LAG, p - LAG)(combine)
 
     @pl.loop(p - LAG, p)
     def _(c):
         received(c)
-        scale = scales(c)
-        for h in range(groups // 2):
-            together(c, h, scale)
+        combine(c)
 
     arrived(stats.at[:, p], 0, p).wait_recv()
     scale = scales(p)
@@ -305,9 +303,8 @@
                 pltpu.SemaphoreType.DMA,
                 pltpu.SemaphoreType.DMA((SLOTS,)),
                 pltpu.SemaphoreType.DMA((SLOTS,)),
-                pltpu.SemaphoreType.DMA((2, groups)),
-                pltpu.SemaphoreType.DMA((3, 2)),
-                pltpu.SemaphoreType.DMA((3, RING)),
+                pltpu.SemaphoreType.DMA((5,)),
+                pltpu.SemaphoreType.DMA((2 * RING + 1,)),
             ],
             compiler_params=pltpu.CompilerParams(collective_id=0, has_side_effects=True, vmem_limit_bytes=48 * 2**20),
         )(q, k, v)

time: 50.2 us -> 48.8 us (0.972)
  Pallas kernels: 49.4 us -> 48 us
    pallas_call x1, Pallas kernels: 49.4 us -> 48 us  [step(): pl.pallas_call(functools.partial(attend, pairs, heads, head), out_shape=j...]
where the time goes in v4:
time: 48.8 us; the launch traced here: 48.7 us
  Pallas kernels  48 us (98%)
  local copies, waits for them, and re-layouts  0.71 us (1%)
    pallas_call x1, Pallas kernels, step(): pl.pallas_call(functools.partial(attend, pairs, heads, head), out_shape=j...  48 us

profile of v4, /device:TPU:0, one launch (start us, length us, event | category | flops | bytes accessed | tf_op | source)
XLA Modules:
  0.0 48.7 jit_solution(17870514099066078437)
XLA Ops:
  0.0 48.0 %shard_map.37 = bf16[32,32,64]{2,1,0:T(8,128)(2,1)S(1)} custom-call(bf16[32,32,64]{2,1,0:T(8,128)(2,1)} %q_hbm.1, bf16[32,2048,512]{2,1,0:T(8,128)(2,1)} %bitcast.1.k_hbm, bf16[32,2048,512]{2,1,0:T(8,128)(2,1)} %bitcast.3.v_hbm), custom_call_target="tpu_custom_call" | custom-call | tf_op jit(solution)/shard_map/pallas_call | solution.py:288
  48.0 0.7 %copy.5 = bf16[32,32,64]{2,1,0:T(8,128)(2,1)} copy(bf16[32,32,64]{2,1,0:T(8,128)(2,1)S(1)} %shard_map.37) | data formatting | bytes 262144

commit v5 on v4

v5 whole, which is shorter than its diff:
```python
import functools

import jax
import jax.numpy as jnp
from jax import lax
from jax.experimental import pallas as pl
from jax.experimental.pallas import tpu as pltpu
from jax.sharding import PartitionSpec as P

MESH = pl.DeviceIdType.MESH
SLOTS = 6
LAG = 4
RING = 2 * LAG
GROUP = 8
SHARED = (3,)
TAIL = 4
PEERS = [(x, y, c) for x in (1, 0) for y in (1, 0) for c in (1, 0)][:-1]


def add(terms):
    return functools.reduce(jnp.add, terms)


def attend(pairs, heads, head, q_hbm, k_hbm, v_hbm, out_ref, q_ref, kbuf, vbuf, raw, weights, part, stat, parts, stats, qsem, ksem, vsem, send, recv):
    batch, groups, lanes, tokens = 2 * pairs, heads // GROUP, 2 * head, kbuf.shape[2]
    rows = GROUP * head
    me = lax.axis_index("sp")
    mx, my, mc = me // 4, (me // 2) % 2, me % 2
    devices = [((mx + x) % 2) * 4 + ((my + y) % 2) * 2 + (mc + c) % 2 for x, y, c in PEERS]

    def kcopy(b):
        return pltpu.make_async_copy(k_hbm.at[b], kbuf.at[b % SLOTS], ksem.at[b % SLOTS])

    def vcopy(b):
        return pltpu.make_async_copy(v_hbm.at[b], vbuf.at[b % SLOTS], vsem.at[b % SLOTS])

    qcopy = pltpu.make_async_copy(q_hbm, q_ref, qsem)
    qcopy.start()
    for b in range(4):
        kcopy(b).start(priority=1)
    for b in range(SLOTS - 2):
        vcopy(b).start(priority=1)
        if b + 4 < SLOTS:
            kcopy(b + 4).start(priority=1)

    barrier = pltpu.get_barrier_semaphore()
    for device in devices:
        pl.semaphore_signal(barrier, inc=1, device_id={"sp": device}, device_id_type=MESH)

    lane = lax.broadcasted_iota(jnp.int32, (GROUP, lanes), 1)
    row = lax.broadcasted_iota(jnp.int32, (GROUP, lanes), 0)
    own = [row == 2 * j + lane // head for j in range(GROUP // 2)]
    odd = (lane // head) == row % 2

    def score(b, i, g):
        query = q_ref[b, g * GROUP : (g + 1) * GROUP, :].astype(jnp.float32)
        query = jnp.concatenate([query, query], 1)
        spread = jnp.concatenate([jnp.where(o, query, 0.0) for o in own], 1).astype(jnp.bfloat16)
        keys = kbuf[b % SLOTS, g * rows : (g + 1) * rows, :]
        raw[i, g * GROUP : (g + 1) * GROUP, :] = jnp.dot(spread, keys, preferred_element_type=jnp.float32)

    def soften(i, stat_tile, place):
        for g in range(groups):
            s = raw[i, g * GROUP : (g + 1) * GROUP, :] * head**-0.5
            high = jnp.max(s, 1, keepdims=True)
            w = jnp.exp(s - high)
            weights[i, g * GROUP : (g + 1) * GROUP, :] = w
            total = jnp.sum(w, 1, keepdims=True)
            at = place + g * 4 + i * 2
            stat_tile = jnp.where(lane == at, high, jnp.where(lane == at + 1, total, stat_tile))
        return stat_tile

    def place_of(p):
        return p % 2 * 4 * groups

    def tile_of(p):
        return jnp.where(p % 2 == 1, stat[p // 2], 0.0)

    def values(b, i, g):
        w = weights[i, g * GROUP : (g + 1) * GROUP, :].astype(jnp.bfloat16)
        block = vbuf[b % SLOTS, g * rows : (g + 1) * rows, :]
        seen = lax.dot_general(w, block, (((1,), (1,)), ((), ())), preferred_element_type=jnp.float32)
        return add(jnp.where(o, seen[:, j * lanes : (j + 1) * lanes], 0.0) for j, o in enumerate(own))

    def values_by_lanes(b, i, g):
        w = weights[i, g * GROUP : (g + 1) * GROUP, :].astype(jnp.bfloat16).astype(jnp.float32)
        seen = []
        for h in range(GROUP):
            at = g * rows + h * head
            block = vbuf[b % SLOTS, at : at + head, :].astype(jnp.float32) * w[h : h + 1]
            block = add(block[:, j * lanes : (j + 1) * lanes] for j in range(tokens // lanes))
            seen.append(jnp.sum(block.T, 0, keepdims=True))
        seen = jnp.concatenate(seen, 0)
        return jnp.where(lane // head == row % 2, jnp.concatenate([seen, seen], 1), 0.0)

    def copies(src, dst, sent, got):
        return [
            pltpu.make_async_remote_copy(
                src_ref=src,
                dst_ref=dst.at[r],
                send_sem=send.at[sent],
                recv_sem=recv.at[got],
                device_id={"sp": device},
                device_id_type=MESH,
            )
            for r, device in enumerate(devices)
        ]

    def all_of(dst, sent, got):
        return pltpu.make_async_remote_copy(
            src_ref=dst,
            dst_ref=dst,
            send_sem=send.at[sent],
            recv_sem=recv.at[got],
            device_id={"sp": devices[0]},
            device_id_type=MESH,
        )

    def half(h):
        return pl.ds(h * 2 * GROUP, 2 * GROUP)

    end = pairs - 1

    def part_message(p):
        return part.at[p], parts.at[:, p], p % 2, p % RING

    def stat_message(p):
        m = p // 2
        return stat.at[m], stats.at[:, m], 2 + m % 2, RING + m % (RING // 2)

    def last_message(h):
        return part.at[end, half(h)], parts.at[:, end, half(h)], 4 + h, RING + RING // 2 + h

    def start(message):
        for copy in copies(*message):
            copy.start()

    def wait_sent(message):
        all_of(*message[1:]).wait_send()

    def wait_got(message):
        all_of(*message[1:]).wait_recv()

    def send_pair(p):
        @pl.when(p >= 2)
        def _():
            wait_sent(part_message(p - 2))

        start(part_message(p))

        def two():
            @pl.when(p >= 4)
            def _():
                wait_sent(stat_message(p - 4))

            start(stat_message(p))

        when_even(p, two)

    def got(p):
        wait_got(part_message(p))
        when_even(p, lambda: wait_got(stat_message(p)))

    def when_even(p, do):
        if isinstance(p, int):
            if p % 2 == 0:
                do()
        else:
            pl.when(p % 2 == 0)(do)

    def scales(p):
        each = [stat[p // 2]] + [stats[r, p // 2] for r in range(len(PEERS))]
        high = functools.reduce(jnp.maximum, each)
        scale = [jnp.exp(e - high) for e in each]
        total = add(pltpu.roll(e, lanes - 1, 1) * s for e, s in zip(each, scale))
        scale = [pltpu.roll(s / total, (lanes - place_of(p)) % lanes, 1) for s in scale]
        return [[jnp.where(odd, s[:, 4 * g + 2 : 4 * g + 3], s[:, 4 * g : 4 * g + 1]) for s in scale] for g in range(groups)]

    def together(p, h, scale):
        piece = slice(h * 2 * GROUP, (h + 1) * 2 * GROUP)
        tiles = [t.astype(jnp.float32) for t in [part[p, piece, :]] + [parts[r, p, piece, :] for r in range(len(PEERS))]]
        result = [[], []]
        for i in range(2):
            both = add(t[i * GROUP : (i + 1) * GROUP] * s for t, s in zip(tiles, scale[2 * h + i]))
            swapped = pltpu.roll(both, head, 1)
            result[0].append(jnp.where(row % 2 == 0, swapped, both)[:, :head])
            result[1].append(jnp.where(row % 2 == 0, both, swapped)[:, :head])
        for i in range(2):
            out_ref[2 * p + i, piece, :] = jnp.concatenate(result[i], 0).astype(out_ref.dtype)

    def store(p, even, odd_tiles, h):
        tile = jnp.concatenate([pltpu.roll(even[g], head, 1) + odd_tiles[g] for g in (2 * h, 2 * h + 1)], 0)
        part[p, h * 2 * GROUP : (h + 1) * 2 * GROUP, :] = tile.astype(part.dtype)

    def attended(b, i, shared=False):
        return [(values_by_lanes if shared and g in SHARED else values)(b, i, g) for g in range(groups)]

    def pair(p, combine):
        b = 2 * p
        for i in range(2):
            vcopy(b + i).wait()
            kcopy(b + i + 4).wait()
        if combine:
            got(p - LAG)
        tiles = [attended(b + i, i) for i in range(2)]
        place = place_of(p + 1)
        stat[(p + 1) // 2] = soften(1, soften(0, tile_of(p + 1), place), place)
        for i in range(2):
            for g in range(groups):
                score(b + i + 4, i, g)
        if combine:
            scale = scales(p - LAG)
            for h in range(groups // 2):
                together(p - LAG, h, scale)
        for h in range(groups // 2):
            store(p, *tiles, h)
        for i in range(2):
            refill(b + i)

    def refill(b):
        @pl.when(b + SLOTS < batch)
        def _():
            vcopy(b + SLOTS).start(priority=1)

        @pl.when(b + 4 + SLOTS < batch)
        def _():
            kcopy(b + 4 + SLOTS).start(priority=1)

    qcopy.wait()
    for i in range(2):
        kcopy(i).wait()
    for i in range(2):
        for g in range(groups):
            score(i, i, g)
    for i in range(2):
        kcopy(i + SLOTS).start(priority=1)
        kcopy(i + 2).wait()
    stat[0] = soften(1, soften(0, jnp.zeros((GROUP, lanes), jnp.float32), 0), 0)
    for i in range(2):
        for g in range(groups):
            score(i + 2, i, g)
    for i in range(2):
        kcopy(i + 2 + SLOTS).start(priority=1)
        vcopy(i + SLOTS - 2).start(priority=1)

    pair(0, False)
    pl.semaphore_wait(barrier, len(PEERS))

    def step(p, combine):
        send_pair(p - 1)
        pair(p, combine)

    @pl.loop(1, LAG)
    def _(p):
        step(p, False)

    @pl.loop(LAG, pairs - TAIL)
    def _(p):
        step(p, True)

    for p in range(pairs - TAIL, pairs - 1):
        send_pair(p - 1)
        got(p - LAG)
        tiles, stat_tile = [], tile_of(p + 1)
        for i in range(2):
            b = 2 * p + i
            vcopy(b).wait()
            if b + 4 < batch:
                kcopy(b + 4).wait()
            tiles.append(attended(b, i, b + 4 >= batch))
            stat_tile = soften(i, stat_tile, place_of(p + 1))
            if b + 4 < batch:
                for g in range(groups):
                    score(b + 4, i, g)
            refill(b)
        stat[(p + 1) // 2] = stat_tile
        for h in range(groups // 2):
            store(p, *tiles, h)

    send_pair(end - 1)
    vcopy(batch - 2).wait()
    even = attended(batch - 2, 0, True)
    vcopy(batch - 1).wait()
    for h in range(groups // 2):
        odd_tiles = {g: (values_by_lanes if g in SHARED else values)(batch - 1, 1, g) for g in (2 * h, 2 * h + 1)}
        store(end, even, odd_tiles, h)
        start(last_message(h))

    def combine(c):
        scale = scales(c)
        for h in range(groups // 2):
            together(c, h, scale)

    pl.loop(pairs - TAIL - LAG, end - LAG)(combine)

    @pl.loop(end - LAG, end)
    def _(c):
        got(c)
        combine(c)

    scale = scales(end)
    for h in range(groups // 2):
        wait_got(last_message(h))
        together(end, h, scale)

    for p in (end - 2, end - 1):
        wait_sent(part_message(p))
    for p in (end - 3, end - 1):
        wait_sent(stat_message(p))
    for h in range(groups // 2):
        wait_sent(last_message(h))


def solution(mesh):
    def step(q, k, v):
        batch, tokens, heads, head = k.shape
        pairs = batch // 2
        k, v = (jnp.transpose(x, (0, 2, 3, 1)).reshape(batch, heads * head, tokens) for x in (k, v))
        q = pltpu.with_memory_space_constraint(q, pltpu.HBM)
        n, groups = len(PEERS), heads // GROUP
        block = pltpu.VMEM((SLOTS, heads * head, tokens), jnp.bfloat16)
        return pl.pallas_call(
            functools.partial(attend, pairs, heads, head),
            out_shape=jax.ShapeDtypeStruct(q.shape, q.dtype),
            in_specs=[pl.BlockSpec(memory_space=pltpu.HBM)] * 3,
            out_specs=pl.BlockSpec(memory_space=pltpu.VMEM),
            scratch_shapes=[
                pltpu.VMEM(q.shape, q.dtype),
                block,
                block,
                pltpu.VMEM((2, heads, tokens), jnp.float32),
                pltpu.VMEM((2, heads, tokens), jnp.float32),
                pltpu.VMEM((pairs, heads, 2 * head), jnp.bfloat16),
                pltpu.VMEM((pairs // 2, GROUP, 2 * head), jnp.float32),
                pltpu.VMEM((n, pairs, heads, 2 * head), jnp.bfloat16),
                pltpu.VMEM((n, pairs // 2, GROUP, 2 * head), jnp.float32),
                pltpu.SemaphoreType.DMA,
                pltpu.SemaphoreType.DMA((SLOTS,)),
                pltpu.SemaphoreType.DMA((SLOTS,)),
                pltpu.SemaphoreType.DMA((4 + groups // 2,)),
                pltpu.SemaphoreType.DMA((RING + RING // 2 + groups // 2,)),
            ],
            compiler_params=pltpu.CompilerParams(collective_id=0, has_side_effects=True, vmem_limit_bytes=48 * 2**20),
        )(q, k, v)

    return jax.shard_map(
        step,
        mesh=mesh,
        in_specs=(P("dp", None, None), P("dp", "sp", None, None), P("dp", "sp", None, None)),
        out_specs=P("dp", None, None),
        check_vma=False,
    )
```

time: 48.8 us -> 47.9 us (0.982)
  Pallas kernels: 48 us -> 47.1 us
    pallas_call x1, Pallas kernels: 48 us -> 47.1 us  [step(): pl.pallas_call(functools.partial(attend, pairs, heads, head), out_shape=j...]
where the time goes in v5:
time: 47.9 us; the launch traced here: 47.8 us
  Pallas kernels  47.1 us (98%)
  local copies, waits for them, and re-layouts  0.71 us (1%)
    pallas_call x1, Pallas kernels, step(): pl.pallas_call(functools.partial(attend, pairs, heads, head), out_shape=j...  47.1 us

profile of v5, /device:TPU:0, one launch (start us, length us, event | category | flops | bytes accessed | tf_op | source)
XLA Modules:
  0.0 47.8 jit_solution(15471418531962306448)
XLA Ops:
  0.0 47.1 %shard_map.37 = bf16[32,32,64]{2,1,0:T(8,128)(2,1)S(1)} custom-call(bf16[32,32,64]{2,1,0:T(8,128)(2,1)} %q_hbm.1, bf16[32,2048,512]{2,1,0:T(8,128)(2,1)} %bitcast.1.k_hbm, bf16[32,2048,512]{2,1,0:T(8,128)(2,1)} %bitcast.3.v_hbm), custom_call_target="tpu_custom_call" | custom-call | tf_op jit(solution)/shard_map/pallas_call | solution.py:322
  47.1 0.7 %copy.5 = bf16[32,32,64]{2,1,0:T(8,128)(2,1)} copy(bf16[32,32,64]{2,1,0:T(8,128)(2,1)S(1)} %shard_map.37) | data formatting | bytes 262144

commit v6 on v5

--- a/solution.py
+++ b/solution.py
@@ -12,7 +12,7 @@
 LAG = 4
 RING = 2 * LAG
 GROUP = 8
-SHARED = (3,)
+SHARED = (1, 3)
 TAIL = 4
 PEERS = [(x, y, c) for x in (1, 0) for y in (1, 0) for c in (1, 0)][:-1]
 
@@ -59,12 +59,12 @@
         keys = kbuf[b % SLOTS, g * rows : (g + 1) * rows, :]
         raw[i, g * GROUP : (g + 1) * GROUP, :] = jnp.dot(spread, keys, preferred_element_type=jnp.float32)
 
-    def soften(i, stat_tile, place):
+    def soften(i, stat_tile, place, to=0):
         for g in range(groups):
             s = raw[i, g * GROUP : (g + 1) * GROUP, :] * head**-0.5
             high = jnp.max(s, 1, keepdims=True)
             w = jnp.exp(s - high)
-            weights[i, g * GROUP : (g + 1) * GROUP, :] = w
+            weights[to + i, g * GROUP : (g + 1) * GROUP, :] = w
             total = jnp.sum(w, 1, keepdims=True)
             at = place + g * 4 + i * 2
             stat_tile = jnp.where(lane == at, high, jnp.where(lane == at + 1, total, stat_tile))
@@ -141,21 +141,23 @@
     def wait_got(message):
         all_of(*message[1:]).wait_recv()
 
-    def send_pair(p):
+    def send_part(p):
         @pl.when(p >= 2)
         def _():
             wait_sent(part_message(p - 2))
 
         start(part_message(p))
 
-        def two():
-            @pl.when(p >= 4)
-            def _():
-                wait_sent(stat_message(p - 4))
-
-            start(stat_message(p))
-
-        when_even(p, two)
+    def send_stat(p):
+        @pl.when(p >= 4)
+        def _():
+            wait_sent(stat_message(p - 4))
+
+        start(stat_message(p))
+
+    def send_pair(p):
+        send_part(p)
+        when_even(p, lambda: send_stat(p))
 
     def got(p):
         wait_got(part_message(p))
@@ -261,28 +263,33 @@
     for p in range(pairs - TAIL, pairs - 1):
         send_pair(p - 1)
         got(p - LAG)
-        tiles, stat_tile = [], tile_of(p + 1)
+        tiles, stat_tile, place = [], tile_of(p + 1), place_of(p + 1)
+        if p == end - 1:
+            stat[p // 2] = soften(1, soften(0, stat_tile, place, 2), place, 2)
+            send_stat(p)
         for i in range(2):
             b = 2 * p + i
             vcopy(b).wait()
             if b + 4 < batch:
                 kcopy(b + 4).wait()
-            tiles.append(attended(b, i, b + 4 >= batch))
-            stat_tile = soften(i, stat_tile, place_of(p + 1))
+            tiles.append(attended(b, i, True))
+            if p < end - 1:
+                stat_tile = soften(i, stat_tile, place)
             if b + 4 < batch:
                 for g in range(groups):
                     score(b + 4, i, g)
             refill(b)
-        stat[(p + 1) // 2] = stat_tile
+        if p < end - 1:
+            stat[(p + 1) // 2] = stat_tile
         for h in range(groups // 2):
             store(p, *tiles, h)
 
-    send_pair(end - 1)
+    send_part(end - 1)
     vcopy(batch - 2).wait()
-    even = attended(batch - 2, 0, True)
+    even = attended(batch - 2, 2, True)
     vcopy(batch - 1).wait()
     for h in range(groups // 2):
-        odd_tiles = {g: (values_by_lanes if g in SHARED else values)(batch - 1, 1, g) for g in (2 * h, 2 * h + 1)}
+        odd_tiles = {g: (values_by_lanes if g in SHARED else values)(batch - 1, 3, g) for g in (2 * h, 2 * h + 1)}
         store(end, even, odd_tiles, h)
         start(last_message(h))
 
@@ -329,7 +336,7 @@
                 block,
                 block,
                 pltpu.VMEM((2, heads, tokens), jnp.float32),
-                pltpu.VMEM((2, heads, tokens), jnp.float32),
+                pltpu.VMEM((4, heads, tokens), jnp.float32),
                 pltpu.VMEM((pairs, heads, 2 * head), jnp.bfloat16),
                 pltpu.VMEM((pairs // 2, GROUP, 2 * head), jnp.float32),
                 pltpu.VMEM((n, pairs, heads, 2 * head), jnp.bfloat16),

time: 47.9 us -> 47.5 us (level)
  no operation moved by 1% of the time
where the time goes in v6:
time: 47.5 us; the launch traced here: 47.4 us
  Pallas kernels  46.7 us (98%)
  local copies, waits for them, and re-layouts  0.71 us (1%)
    pallas_call x1, Pallas kernels, step(): pl.pallas_call(functools.partial(attend, pairs, heads, head), out_shape=j...  46.7 us

profile of v6, /device:TPU:0, one launch (start us, length us, event | category | flops | bytes accessed | tf_op | source)
XLA Modules:
  0.0 47.4 jit_solution(11321230095818690508)
XLA Ops:
  0.0 46.7 %shard_map.37 = bf16[32,32,64]{2,1,0:T(8,128)(2,1)S(1)} custom-call(bf16[32,32,64]{2,1,0:T(8,128)(2,1)} %q_hbm.1, bf16[32,2048,512]{2,1,0:T(8,128)(2,1)} %bitcast.1.k_hbm, bf16[32,2048,512]{2,1,0:T(8,128)(2,1)} %bitcast.3.v_hbm), custom_call_target="tpu_custom_call" | custom-call | tf_op jit(solution)/shard_map/pallas_call | solution.py:329
  46.7 0.7 %copy.5 = bf16[32,32,64]{2,1,0:T(8,128)(2,1)} copy(bf16[32,32,64]{2,1,0:T(8,128)(2,1)S(1)} %shard_map.37) | data formatting | bytes 262144

commit v7 on v6

--- a/solution.py
+++ b/solution.py
@@ -14,7 +14,7 @@
 GROUP = 8
 SHARED = (1, 3)
 TAIL = 4
-PEERS = [(x, y, c) for x in (1, 0) for y in (1, 0) for c in (1, 0)][:-1]
+PEERS = [(1, 1, 0), (1, 1, 1), (1, 0, 0), (0, 1, 0), (1, 0, 1), (0, 1, 1), (0, 0, 1)]
 
 
 def add(terms):

time: 47.5 us -> 47.4 us (level)
  no operation moved by 1% of the time
where the time goes in v7:
time: 47.4 us
  Pallas kernels  46.6 us (98%)
  local copies, waits for them, and re-layouts  0.71 us (1%)
    pallas_call x1, Pallas kernels, step(): pl.pallas_call(functools.partial(attend, pairs, heads, head), out_shape=j...  46.6 us

profile of v7, /device:TPU:0, one launch (start us, length us, event | category | flops | bytes accessed | tf_op | source)
XLA Modules:
  0.0 47.4 jit_solution(9918058865901626730)
XLA Ops:
  0.0 46.6 %shard_map.37 = bf16[32,32,64]{2,1,0:T(8,128)(2,1)S(1)} custom-call(bf16[32,32,64]{2,1,0:T(8,128)(2,1)} %q_hbm.1, bf16[32,2048,512]{2,1,0:T(8,128)(2,1)} %bitcast.1.k_hbm, bf16[32,2048,512]{2,1,0:T(8,128)(2,1)} %bitcast.3.v_hbm), custom_call_target="tpu_custom_call" | custom-call | tf_op jit(solution)/shard_map/pallas_call | solution.py:329
  46.6 0.7 %copy.5 = bf16[32,32,64]{2,1,0:T(8,128)(2,1)} copy(bf16[32,32,64]{2,1,0:T(8,128)(2,1)S(1)} %shard_map.37) | data formatting | bytes 262144
